TPU v7x, 8 devices: a whole 2x2x1 slice. The times are simulated.
8 devices in a mesh: nodes: 8 (over z, y, x, core).
Axes of the slice: x: 2, y: 2, z: 1, core: 2. Of those that a mesh axis runs over, the one named last changes fastest.
Arguments:
- adjacency: bfloat16 [16384, 16384], P('nodes')
- features: bfloat16 [16384, 100], P('nodes')
- w_one: float32 [100, 128], replicated
- w_two: float32 [128, 47], replicated
- labels: int32 [16384], P('nodes')
- label_mask: int32 [16384], P('nodes')
Outputs:
- output 1: float32 [1], replicated
- output 2: float32 [100, 128], replicated
- output 3: float32 [128, 47], replicated
All inputs are finite; a program needn't handle non-finite values.
Results may differ from a plain program's by a relative error of at most 0.001.
Values are sent between devices in bfloat16 or wider.
A program may use at most 1 GiB of HBM per device.

v0:
```python
import jax
import jax.numpy as jnp
from jax import lax
from jax.sharding import PartitionSpec as P

ROW_CONTRACT = (((0,), (0,)), ((), ()))
COL_CONTRACT = (((1,), (1,)), ((), ()))


def solution(mesh):
    axis_name = 'nodes'

    def local_step(adj_rows, feat_rows, w_one, w_two, label_rows, mask_rows):
        weight_one = w_one.astype(jnp.bfloat16)
        weight_two = w_two.astype(jnp.bfloat16)
        num_classes = w_two.shape[1]
        feats_all = lax.all_gather(feat_rows, axis_name, tiled=True)
        agg_one = jnp.dot(adj_rows, feats_all, preferred_element_type=jnp.float32).astype(jnp.bfloat16)
        pre_one = jnp.dot(agg_one, weight_one, preferred_element_type=jnp.float32)
        hidden = jnp.maximum(pre_one, 0.0).astype(jnp.bfloat16)
        hidden_all = lax.all_gather(hidden, axis_name, tiled=True)
        agg_two = jnp.dot(adj_rows, hidden_all, preferred_element_type=jnp.float32).astype(jnp.bfloat16)
        logits = jnp.dot(agg_two, weight_two, preferred_element_type=jnp.float32)
        weight = mask_rows.astype(jnp.float32)
        label_count = lax.psum(jnp.sum(weight), axis_name)
        onehot = (label_rows[:, None] == jnp.arange(num_classes)[None, :]).astype(jnp.float32)
        log_prob = jax.nn.log_softmax(logits, axis=-1)
        loss_sum = lax.psum(-jnp.sum(weight * jnp.sum(onehot * log_prob, axis=-1)), axis_name)
        grad_two = (weight[:, None] * (jnp.exp(log_prob) - onehot) / label_count).astype(jnp.bfloat16)
        dw_two = lax.psum(lax.dot_general(agg_two, grad_two, ROW_CONTRACT, preferred_element_type=jnp.float32), axis_name)
        back_two = lax.dot_general(grad_two, weight_two, COL_CONTRACT, preferred_element_type=jnp.float32).astype(jnp.bfloat16)
        part_sums = lax.dot_general(adj_rows, back_two, ROW_CONTRACT, preferred_element_type=jnp.float32)
        d_hidden = lax.psum_scatter(part_sums, axis_name, scatter_dimension=0, tiled=True)
        grad_one = jnp.where(pre_one > 0.0, d_hidden, 0.0).astype(jnp.bfloat16)
        dw_one = lax.psum(lax.dot_general(agg_one, grad_one, ROW_CONTRACT, preferred_element_type=jnp.float32), axis_name)
        return ((loss_sum / label_count).reshape(1), dw_one, dw_two)

    return jax.shard_map(local_step, mesh=mesh, in_specs=(P(axis_name, None), P(axis_name, None), P(None, None), P(None, None), P(axis_name), P(axis_name)), out_specs=(P(None), P(None, None), P(None, None)), check_vma=False)
```

profile of v0, /device:TPU:0, one launch (start us, length us, event | category | flops | bytes accessed | tf_op | source)
XLA Modules:
  0.0 288.3 jit_solution(7963522680277801475)
XLA Ops:
  7.2 0.0 copy-start.1
  7.2 0.0 copy-start.3
  7.2 0.0 all-gather.3.cloned.1.call-start
  7.2 0.7 all-gather.3.cloned.1.call-update
  7.9 0.0 all-gather.5.cloned.1.call-start
  8.0 32.2 %all-gather.3.cloned.1.call-done = bf16[16384,100]{0,1:T(8,128)(2,1)} async-done(((bf16[2048,100]{0,1:T(8,128)(2,1)}), bf16[16384,100]{0,1:T(8,128)(2,1)}) %all-gather.3.cloned.1.call-update) | async-done | bytes 3276816 | tf_op jit(solution)/shard_map/all_gather | solution.py:17
  40.1 29.5 %convolution_convert_fusion.2 = bf16[2048,100]{0,1:T(8,128)(2,1)S(1)} fusion(bf16[2048,16384]{1,0:T(8,128)(2,1)} %param.6, bf16[16384,100]{0,1:T(8,128)(2,1)} %all-gather.3.cloned.1.call-done), kind=kOutput, calls=%fused_computation.3 | convolution fusion | flops 6711091200 | bytes 70795264 | tf_op jit(solution)/shard_map/dot_general | solution.py:18
  69.6 1.2 maximum_convert_fusion
  70.8 0.0 all-gather.5.cloned.1.call-update
  70.8 0.0 reduce-scatter.2.cloned.1.call-start
  70.9 30.8 %all-gather.5.cloned.1.call-done = bf16[16384,128]{1,0:T(8,128)(2,1)} async-done(((bf16[2048,128]{1,0:T(8,128)(2,1)}), bf16[16384,128]{1,0:T(8,128)(2,1)}) %all-gather.5.cloned.1.call-update) | async-done | bytes 4194320 | tf_op jit(solution)/shard_map/all_gather | solution.py:21
  101.7 29.0 %convolution_convert_fusion.1 = bf16[128,2048]{1,0:T(8,128)(2,1)S(1)} fusion(bf16[16384,128]{1,0:T(8,128)(2,1)} %all-gather.5.cloned.1.call-done, bf16[2048,16384]{1,0:T(8,128)(2,1)} %param.6), kind=kOutput, calls=%fused_computation.2 | convolution fusion | flops 8590196736 | bytes 71827456 | tf_op jit(solution)/shard_map/dot_general | solution.py:22
  130.7 0.2 fusion.9
  130.9 0.1 exponential_reduce_fusion
  131.0 0.1 select_reduce_fusion
  131.1 0.6 convert_reduce_fusion
  131.7 22.6 %psum.29 = f32[]{:T(128)} all-reduce(f32[]{:T(128)} %get-tuple-element.3), channel_id=1, replica_groups=mesh['nodes'=8] {'nodes'}, use_global_device_ids=true, to_apply=%region_6.7 | all-reduce | flops 1 | bytes 8 | tf_op jit(solution)/shard_map/psum | solution.py:25
  154.3 0.8 divide_convert_fusion
  155.1 34.2 %convolution_bitcast_fusion = f32[16384,128]{1,0:T(8,128)} fusion(bf16[2048,16384]{1,0:T(8,128)(2,1)} %param.6, bf16[2048,47]{0,1:T(8,128)(2,1)S(1)} %divide_convert_fusion, f32[128,47]{0,1:T(8,128)S(1)} %copy-done), kind=kOutput, calls=%fused_computation | convolution fusion | flops 8614844416 | bytes 75714048 | tf_op jit(solution)/shard_map/dot_general | solution.py:32
  189.3 0.0 reduce-scatter.2.cloned.1.call-update
  190.0 0.3 fusion.10
  190.3 63.4 %reduce-scatter.2.cloned.1.call-done = f32[2048,128]{1,0:T(8,128)} async-done(((f32[16384,128]{1,0:T(8,128)}), f32[2048,128]{1,0:T(8,128)}) %reduce-scatter.2.cloned.1.call-update) | async-done | bytes 1048592 | tf_op jit(solution)/shard_map/reduce_scatter | solution.py:33
  253.7 1.5 fusion
  255.2 24.0 %all-reduce.2 = (f32[]{:T(128)}, f32[100,128]{1,0:T(8,128)}, f32[128,47]{0,1:T(8,128)}) all-reduce(f32[]{:T(128)S(6)} %neg.3, f32[100,128]{1,0:T(8,128)S(1)} %fusion, f32[128,47]{0,1:T(8,128)S(1)} %fusion.10), channel_id=1, replica_groups=mesh['nodes'=8] {'nodes'}, use_global_device_ids=true, to_apply=%region_4.5 | all-reduce | flops 18817 | bytes 150536 | tf_op jit(solution)/shard_map/psum | solution.py:28
  (8 shorter events, 0.0 us)
Async XLA Ops:
  7.2 62.5 %copy-start.1 = (f32[100,128]{1,0:T(8,128)S(1)}, f32[100,128]{1,0:T(8,128)}, u32[]{:S(2)}) copy-start(f32[100,128]{1,0:T(8,128)} %param.8) | copy-start | bytes 153604
  7.2 63.7 %copy-start.3 = (s32[2048]{0:T(1024)S(1)}, s32[2048]{0:T(1024)}, u32[]{:S(2)}) copy-start(s32[2048]{0:T(1024)} %param.11) | copy-start | bytes 24580
  7.2 33.0 %all-gather.3.cloned.1.call-start = ((), (), s32[]{:S(2)}) async-start(), calls=%async_computation.1 | async-start | bytes 3833856 | tf_op jit(solution)/shard_map/all_gather | solution.py:17
  7.9 122.7 %copy-start = (f32[128,47]{0,1:T(8,128)S(1)}, f32[128,47]{0,1:T(8,128)}, u32[]{:S(2)}) copy-start(f32[128,47]{0,1:T(8,128)} %param.9) | copy-start | bytes 72196
  7.9 123.1 %copy-start.2 = (s32[2048]{0:T(1024)S(1)}, s32[2048]{0:T(1024)}, u32[]{:S(2)}) copy-start(s32[2048]{0:T(1024)} %param.10) | copy-start | bytes 24580
  7.9 93.8 %all-gather.5.cloned.1.call-start = ((), (), s32[]{:S(2)}) async-start(), calls=%async_computation.2 | async-start | bytes 4718592 | tf_op jit(solution)/shard_map/all_gather | solution.py:21
  70.8 182.9 %reduce-scatter.2.cloned.1.call-start = ((), (), s32[]{:S(2)}) async-start(), calls=%async_computation.3 | async-start | bytes 9437184 | tf_op jit(solution)/shard_map/reduce_scatter | solution.py:33
Sparse Core Ops, SparseCore 0:
  9.8 30.2 all-gather.2
  70.9 30.7 all-gather.4
  189.5 64.1 reduce-scatter.1
where the time goes:
time: 289 us; the launch traced here: 288 us
  waiting for transfers between devices  127 us (44%)
  matrix products  95.8 us (33%)
  blocking collectives  46.6 us (16%)
  between operations  17 us (6%)
    reduce_scatter x1, waiting for transfers between devices, local_step(): lax.psum_scatter(part_sums, axis_name, scatter_dimension=0, tiled=True)  63.4 us
    dot_general x1, matrix products, local_step(): lax.dot_general(adj_rows, back_two, ROW_CONTRACT, preferred_element_type=...  34.2 us
    all_gather x1, waiting for transfers between devices, local_step(): feats_all = lax.all_gather(feat_rows, axis_name, tiled=True)  32.2 us
    all_gather x1, waiting for transfers between devices, local_step(): hidden_all = lax.all_gather(hidden, axis_name, tiled=True)  30.8 us
    dot_general x1, matrix products, local_step(): jnp.dot(adj_rows, feats_all, preferred_element_type=jnp.float32)  29.5 us
    dot_general x1, matrix products, local_step(): jnp.dot(adj_rows, hidden_all, preferred_element_type=jnp.float32)  29 us
    psum x1, blocking collectives, local_step(): lax.psum(-jnp.sum(weight * jnp.sum(onehot * log_prob, axis=-1)), axis_name)  24 us
    psum x1, blocking collectives, local_step(): label_count = lax.psum(jnp.sum(weight), axis_name)  22.6 us
  transfers between devices with their start and end apart: 3, of which 3 were waited for; matrix products, arithmetic and copies ran while one was open for 0% of the time, Pallas kernels for 0%

commit v1 on v0

v1 whole, which is shorter than its diff:
```python
import jax
import jax.numpy as jnp
from jax import lax
from jax.experimental import pallas as pl
from jax.experimental.pallas import tpu as pltpu
from jax.sharding import PartitionSpec as P

MESH = pl.DeviceIdType.MESH
F32, BF16 = jnp.float32, jnp.bfloat16
LANE_CONTRACT = (((1,), (1,)), ((), ()))

ROWS = 2048
TILE = 1024
SLOTS = 8
FEAT = 104
HID = 128
CLS = 48
RED = FEAT + CLS + 8


def kernel(adj, feat, w1t, w2t, w2, label, mask, mask_any, out,
           ring, xbuf, sbuf, acc1, acc2, hid, s2t, ut, mall, dcls,
           pbuf, rbuf, cbuf, rsbuf, red, redp, half, fin,
           ring_sem, loc_sem, ag_send, ag_recv, m_send, m_recv,
           d_send, d_recv, rs_send, rs_recv, f_send, f_recv):
    me = lax.axis_index('nodes')
    core, px, py = me % 2, (me // 2) % 2, me // 4

    def device(fy, fx, fc):
        return 4 * ((py + fy) % 2) + 2 * ((px + fx) % 2) + (core + fc) % 2

    partner, xn, yn, diag = device(0, 0, 1), device(0, 1, 0), device(1, 0, 0), device(1, 1, 0)

    def columns(u):
        s, back = u % 16, u // 32
        g = (1 - back) * (s // 4) + back * (3 - s // 4)
        r = (1 - back) * (s % 2) + back * ((s // 2) % 2)
        fc = (1 - back) * ((s // 2) % 2) + back * (1 - s % 2)
        t = (g + 1) // 2
        fx, fy = (t + 1 - r) // 2, (t + r) // 2
        h = (r + (g // 2) * (3 - g)) % 2
        return pl.multiple_of(device(fy, fx, fc) * ROWS + h * TILE, TILE)

    def tile(u):
        slot = u % SLOTS
        return pltpu.make_async_copy(adj.at[:, pl.ds(columns(u), TILE)], ring.at[slot], ring_sem.at[slot])

    def remote(src, dst, ssem, rsem, dev):
        return pltpu.make_async_remote_copy(src_ref=src, dst_ref=dst, send_sem=ssem, recv_sem=rsem,
                                            device_id=(dev,), device_id_type=MESH)

    for u in range(SLOTS):
        tile(u).start()
    own = [pltpu.make_async_copy(feat.at[:, pl.ds(h * TILE, TILE)], xbuf.at[h], loc_sem.at[h]) for h in range(2)]
    own.append(pltpu.make_async_copy(mask_any, mall.at[0], loc_sem.at[2]))
    for c in own:
        c.start()

    peers = [device(e // 4, (e // 2) % 2, e % 2) for e in range(8)]
    barrier = pltpu.get_barrier_semaphore()
    for e in range(1, 8):
        pl.semaphore_signal(barrier, inc=1, device_id=(peers[e],), device_id_type=MESH)
    pl.semaphore_wait(barrier, 7)

    def gather_copy(ph, buf, src, step, dev):
        return remote(src, buf.at[step], ag_send.at[ph, step], ag_recv.at[ph, step], dev)

    def gather_start(ph, buf, srcs):
        for step, h, dev in ((4, 0, xn), (5, 1, yn), (2, 0, partner), (3, 1, partner), (8, 1, xn), (9, 0, yn)):
            gather_copy(ph, buf, srcs[h], step, dev).start()

    def gather_step(ph, buf, s):
        @pl.when(s >= 2)
        def _():
            gather_copy(ph, buf, buf.at[s], s, partner).wait_recv()

        @pl.when((s >= 4) & (s % 4 < 2))
        def _():
            gather_copy(ph, buf, buf.at[s], s + 2, partner).start()

        @pl.when(s == 4)
        def _():
            gather_copy(ph, buf, buf.at[s], 12, yn).start()

        @pl.when(s == 5)
        def _():
            gather_copy(ph, buf, buf.at[s], 13, xn).start()

    def gather_finish(ph, buf):
        for step in range(2, 16):
            gather_copy(ph, buf, buf.at[0], step, partner).wait_send()

    gather_start(0, xbuf, [feat.at[:, pl.ds(h * TILE, TILE)] for h in range(2)])
    m_copies = [remote(mask_any, mall.at[e], m_send.at[e], m_recv.at[e], peers[e]) for e in range(1, 8)]
    for c in m_copies:
        c.start()
    for c in own:
        c.wait()

    acc1[...] = jnp.zeros_like(acc1)

    def first(s, _):
        tile(s).wait()
        gather_step(0, xbuf, s)
        acc1[...] += lax.dot_general(xbuf[s], ring[s % SLOTS], LANE_CONTRACT, preferred_element_type=F32)
        tile(s + SLOTS).start()
        return 0

    lax.fori_loop(0, 16, first, 0)
    for h in range(2):
        sbuf[h] = acc1[:, h * TILE:(h + 1) * TILE].astype(BF16)
    gather_start(1, sbuf, [sbuf.at[h] for h in range(2)])

    acc2[...] = jnp.zeros_like(acc2)

    def second(s, _):
        tile(s + 16).wait()
        gather_step(1, sbuf, s)
        hid[...] = jnp.maximum(jnp.dot(w1t[...], sbuf[s], preferred_element_type=F32), 0.0).astype(BF16)
        acc2[...] += lax.dot_general(hid[...], ring[s % SLOTS], LANE_CONTRACT, preferred_element_type=F32)
        tile(s + 16 + SLOTS).start()
        return 0

    lax.fori_loop(0, 16, second, 0)

    for c in m_copies:
        c.wait()
    count = jnp.sum(jnp.sum(mall[...], axis=0))
    classes = lax.broadcasted_iota(jnp.int32, (CLS, 512), 0)

    def heads(i, loss):
        cols = pl.ds(pl.multiple_of(i * 512, 512), 512)
        agg = acc2[:, cols].astype(BF16)
        s2t[:, cols] = agg
        z = jnp.dot(w2t[...], agg, preferred_element_type=F32)
        z = jnp.where(classes < 47, z, -1e30)
        z = z - jnp.max(z, axis=0, keepdims=True)
        logp = z - jnp.log(jnp.sum(jnp.exp(z), axis=0, keepdims=True))
        onehot = (label[:, cols] == classes).astype(F32)
        weight = mask[:, cols]
        g2 = (weight * (jnp.exp(logp) - onehot) / count).astype(BF16)
        dcls[:, cols] = g2
        ut[:, cols] = jnp.dot(w2[...], g2, preferred_element_type=F32).astype(BF16)
        return loss + weight * jnp.sum(jnp.where(label[:, cols] == classes, logp, 0.0), axis=0, keepdims=True)

    loss = lax.fori_loop(0, ROWS // 512, heads, jnp.zeros((1, 512), F32))

    to_y = (True, False, False, True, False, True)

    def pair_copy(j):
        return remote(pbuf.at[j], rbuf.at[j], d_send.at[j], d_recv.at[j], partner)

    def link_copy(j):
        return remote(cbuf.at[j], rsbuf.at[j], rs_send.at[j], rs_recv.at[j], yn if to_y[j] else xn)

    def finalize(j):
        pair_copy(j).wait_recv()
        if j in (4, 5):
            link_copy(j - 4).wait_recv()
            cbuf[j] = (cbuf[j] + rbuf[j]) + rsbuf[j - 4]
        else:
            cbuf[j] = cbuf[j] + rbuf[j]
        if j < 6:
            link_copy(j).start()

    def third(j, _):
        u = 32 + 2 * j
        tile(u).wait()
        pbuf[j] = jnp.dot(ut[...], ring[u % SLOTS], preferred_element_type=F32)
        pair_copy(j).start()

        @pl.when(j < 4)
        def _():
            tile(u + SLOTS).start()

        tile(u + 1).wait()
        cbuf[j] = jnp.dot(ut[...], ring[(u + 1) % SLOTS], preferred_element_type=F32)

        @pl.when(j < 4)
        def _():
            tile(u + 1 + SLOTS).start()

        for jj in range(7):
            @pl.when(j == jj + 1)
            def _(jj=jj):
                finalize(jj)
        return 0

    lax.fori_loop(0, 8, third, 0)
    finalize(7)

    red[FEAT:FEAT + CLS, :] = lax.dot_general(dcls[...], s2t[...], LANE_CONTRACT, preferred_element_type=F32)
    red[FEAT + CLS:, :] = jnp.broadcast_to(-jnp.sum(loss), (8, HID))
    gather_finish(0, xbuf)
    gather_finish(1, sbuf)
    for j in range(8):
        pair_copy(j).wait_send()

    dw1 = jnp.zeros((FEAT, HID), F32)
    for h, (a, b) in enumerate(((3, 4), (2, 5))):
        z1 = jnp.dot(w1t[...], sbuf[h], preferred_element_type=F32)
        link_copy(a).wait_recv()
        link_copy(b).wait_recv()
        g1 = jnp.where(z1 > 0.0, (cbuf[6 + h] + rsbuf[a]) + rsbuf[b], 0.0).astype(BF16)
        dw1 = dw1 + lax.dot_general(sbuf[h], g1, LANE_CONTRACT, preferred_element_type=F32)
    red[:FEAT, :] = dw1
    for j in range(6):
        link_copy(j).wait_send()

    c0 = remote(red, redp, f_send.at[0], f_recv.at[0], partner)
    c0.start()
    c0.wait()
    rows = pl.ds(pl.multiple_of(core * (RED // 2), 8), RED // 2)
    half[0] = red[rows, :] + redp[rows, :]
    copies = [remote(half.at[0], half.at[e], f_send.at[e], f_recv.at[e], dev) for e, dev in ((1, xn), (2, yn), (3, diag))]
    for c in copies:
        c.start()
    for c in copies:
        c.wait()
    fin[rows, :] = (half[0] + half[1]) + (half[2] + half[3])
    c4 = remote(fin.at[rows], fin.at[rows], f_send.at[4], f_recv.at[4], partner)
    c4.start()
    c4.wait()
    out[:FEAT + CLS, :] = fin[:FEAT + CLS, :]
    out[FEAT + CLS:, :] = fin[FEAT + CLS:, :] / count


def solution(mesh):
    vmem, anywhere = pl.BlockSpec(memory_space=pltpu.VMEM), pl.BlockSpec(memory_space=pl.ANY)

    def local_step(adj, feat, w_one, w_two, label, mask):
        feat_t = jnp.pad(feat.T, ((0, FEAT - 100), (0, 0)))
        w1t = jnp.pad(w_one.astype(BF16).T, ((0, 0), (0, FEAT - 100)))
        w2 = jnp.pad(w_two.astype(BF16), ((0, 0), (0, 1)))
        mask_row = mask.astype(F32).reshape(1, ROWS)
        out = pl.pallas_call(
            kernel,
            out_shape=jax.ShapeDtypeStruct((RED, HID), F32),
            in_specs=[anywhere, anywhere, vmem, vmem, vmem, vmem, vmem, anywhere],
            out_specs=vmem,
            scratch_shapes=[
                pltpu.VMEM((SLOTS, ROWS, TILE), BF16),
                pltpu.VMEM((16, FEAT, TILE), BF16),
                pltpu.VMEM((16, FEAT, TILE), BF16),
                pltpu.VMEM((FEAT, ROWS), F32),
                pltpu.VMEM((HID, ROWS), F32),
                pltpu.VMEM((HID, TILE), BF16),
                pltpu.VMEM((HID, ROWS), BF16),
                pltpu.VMEM((HID, ROWS), BF16),
                pltpu.VMEM((8, 1, ROWS), F32),
                pltpu.VMEM((CLS, ROWS), BF16),
                pltpu.VMEM((8, HID, TILE), F32),
                pltpu.VMEM((8, HID, TILE), F32),
                pltpu.VMEM((8, HID, TILE), F32),
                pltpu.VMEM((6, HID, TILE), F32),
                pltpu.VMEM((RED, HID), F32),
                pltpu.VMEM((RED, HID), F32),
                pltpu.VMEM((4, RED // 2, HID), F32),
                pltpu.VMEM((RED, HID), F32),
                pltpu.SemaphoreType.DMA((SLOTS,)),
                pltpu.SemaphoreType.DMA((3,)),
                pltpu.SemaphoreType.DMA((2, 16)),
                pltpu.SemaphoreType.DMA((2, 16)),
                pltpu.SemaphoreType.DMA((8,)),
                pltpu.SemaphoreType.DMA((8,)),
                pltpu.SemaphoreType.DMA((8,)),
                pltpu.SemaphoreType.DMA((8,)),
                pltpu.SemaphoreType.DMA((6,)),
                pltpu.SemaphoreType.DMA((6,)),
                pltpu.SemaphoreType.DMA((5,)),
                pltpu.SemaphoreType.DMA((5,)),
            ],
            compiler_params=pltpu.CompilerParams(collective_id=0, has_side_effects=True, vmem_limit_bytes=67043328),
            name='gcn_step',
        )(adj, feat_t, w1t, w2.T, w2, label.reshape(1, ROWS), mask_row, mask_row)
        return (out[FEAT + CLS, :1], out[:100], out[FEAT:FEAT + 47].T)

    return jax.shard_map(local_step, mesh=mesh, in_specs=(P('nodes', None), P('nodes', None), P(None, None), P(None, None), P('nodes'), P('nodes')), out_specs=(P(None), P(None, None), P(None, None)), check_vma=False)
```

time: 289 us -> 127 us (0.44)
  waiting for transfers between devices: 127 us -> 0 us
  Pallas kernels: 0 us -> 115 us
  matrix products: 95.8 us -> 0 us
  blocking collectives: 46.6 us -> 0 us
  between operations: 17 us -> 0.65 us
  local copies, waits for them, and re-layouts: 0.02 us -> 7.96 us
    pallas_call x0 -> x1, Pallas kernels: none -> 115 us  [local_step(): pl.pallas_call(kernel, out_shape=jax.ShapeDtypeStruct((RED, HID), F32), i...]
    dot_general x7 -> x0, matrix products: 95.8 us -> none  [the longest x1 34.2 us: local_step(): lax.dot_general(adj_rows, back_two, ROW_CONTRACT, preferred_element_type=...]
    reduce_scatter x1 -> x0, waiting for transfers between devices: 63.4 us -> none  [local_step(): lax.psum_scatter(part_sums, axis_name, scatter_dimension=0, tiled=True)]
    all_gather x2 -> x0, waiting for transfers between devices: 63 us -> none  [the longest x1 32.2 us: local_step(): feats_all = lax.all_gather(feat_rows, axis_name, tiled=True)]
    psum x2 -> x0, blocking collectives: 46.6 us -> none  [the longest x1 24 us: local_step(): lax.psum(-jnp.sum(weight * jnp.sum(onehot * log_prob, axis=-1)), axis_name)]
    pad x0 -> x3, local copies, waits for them, and re-layouts: none -> 3.06 us  [the longest x1 1.81 us: local_step(): feat_t = jnp.pad(feat.T, ((0, FEAT - 100), (0, 0)))]
  transfers between devices with their start and end apart: 3 -> 0, of which waited for: 3 -> 0; matrix products, arithmetic and copies ran while one was open for 0% -> 0% of each run, Pallas kernels for 0% -> 0%
where the time goes in v1:
time: 127 us; the launch traced here: 126 us
  Pallas kernels  115 us (91%)
  local copies, waits for them, and re-layouts  7.96 us (6%)
  other arithmetic  2.85 us (2%)
    pallas_call x1, Pallas kernels, local_step(): pl.pallas_call(kernel, out_shape=jax.ShapeDtypeStruct((RED, HID), F32), i...  115 us
    slice x2, local copies, waits for them, and re-layouts, local_step(): return (out[FEAT + CLS, :1], out[:100], out[FEAT:FEAT + 47].T)  2.63 us

profile of v1, /device:TPU:0, one launch (start us, length us, event | category | flops | bytes accessed | tf_op | source)
XLA Modules:
  0.0 126.3 jit_solution(16813852690802962935)
XLA Ops:
  0.6 1.3 %convert_element_type.17 = f32[2048]{0:T(1024)} convert(s32[2048]{0:T(1024)} %param.11) | non-fusion elementwise | flops 2048 | bytes 16384 | tf_op jit(solution)/shard_map/convert_element_type | solution.py:235
  1.9 0.7 convert_element_type.16
  2.7 0.1 copy.13
  2.8 0.8 convert_element_type.15
  3.6 0.1 copy.12
  3.7 0.6 pad.13.w1t
  4.4 0.6 fusion
  5.0 0.7 copy.14.w2t
  5.7 1.8 %pad.12.feat = bf16[104,2048]{1,0:T(8,128)(2,1)} pad(bf16[100,2048]{1,0:T(8,128)(2,1)} %bitcast.9, bf16[]{:T(256)} %constant.2.clone.1), padding=0_4x0_0 | pad | bytes 835586 | tf_op jit(solution)/shard_map/jit(_pad)/pad | solution.py:232
  7.5 114.8 %gcn_step.1 = f32[160,128]{1,0:T(8,128)} custom-call(bf16[2048,16384]{1,0:T(8,128)(2,1)} %adj.1, bf16[104,2048]{1,0:T(8,128)(2,1)} %pad.12.feat, bf16[128,104]{1,0:T(8,128)(2,1)} %pad.13.w1t, bf16[48,128]{1,0:T(8,128)(2,1)} %copy.14.w2t, bf16[128,48]{1,0:T(8,128)(2,1)} %get-tuple-element.3.w2, s32[1,2048]{1,0:T(1,128)} %bitcast.13, f32[1,2048]{1,0:T(1,128)} %bitcast.11, ...), custom_call_target="tpu_custom_call" | custom-call | tf_op jit(solution)/shard_map/gcn_step/pallas_call | solution.py:236
  122.3 1.2 slice.9
  123.5 1.3 %slice_bitcast_fusion = f32[128,47]{0,1:T(8,128)} fusion(f32[160,128]{1,0:T(8,128)} %gcn_step.1), kind=kLoop, calls=%fused_computation | loop fusion | bytes 48128 | tf_op jit(solution)/shard_map/transpose | solution.py:276
  124.8 1.4 %slice.10 = f32[100,128]{1,0:T(8,128)} slice(f32[160,128]{1,0:T(8,128)} %gcn_step.1), slice={[0:100], [0:128]} | slice | bytes 102400 | tf_op jit(solution)/shard_map/slice | solution.py:276

commit v2 on v1

--- a/solution.py
+++ b/solution.py
@@ -18,8 +18,8 @@
 RED = FEAT + CLS + 8
 
 
-def kernel(adj, feat, w1t, w2t, w2, label, mask, mask_any, out,
-           ring, xbuf, sbuf, acc1, acc2, hid, s2t, ut, mall, dcls,
+def kernel(adj, feat, w_one, w_two_t, label, mask, mask_any, out,
+           w1t, w2t, w2, ring, xbuf, sbuf, acc1, acc2, hid, s2t, ut, mall, dcls,
            pbuf, rbuf, cbuf, rsbuf, red, redp, half, fin,
            ring_sem, loc_sem, ag_send, ag_recv, m_send, m_recv,
            d_send, d_recv, rs_send, rs_recv, f_send, f_recv):
@@ -56,11 +56,19 @@
     for c in own:
         c.start()
 
+    w1t[...] = jnp.concatenate([w_one[...], jnp.zeros((28, HID), F32)], 0).T[:, :FEAT].astype(BF16)
+    wide = jnp.concatenate([w_two_t[...], jnp.zeros((81, HID), F32)], 0)
+    w2t[...] = wide[:CLS].astype(BF16)
+    w2[...] = wide.T[:, :CLS].astype(BF16)
+    acc1[...] = jnp.zeros_like(acc1)
+    acc2[...] = jnp.zeros_like(acc2)
+
     peers = [device(e // 4, (e // 2) % 2, e % 2) for e in range(8)]
     barrier = pltpu.get_barrier_semaphore()
     for e in range(1, 8):
         pl.semaphore_signal(barrier, inc=1, device_id=(peers[e],), device_id_type=MESH)
-    pl.semaphore_wait(barrier, 7)
+    with jax.named_scope('barrier'):
+        pl.semaphore_wait(barrier, 7)
 
     def gather_copy(ph, buf, src, step, dev):
         return remote(src, buf.at[step], ag_send.at[ph, step], ag_recv.at[ph, step], dev)
@@ -97,35 +105,38 @@
     for c in own:
         c.wait()
 
-    acc1[...] = jnp.zeros_like(acc1)
 
     def first(s, _):
-        tile(s).wait()
-        gather_step(0, xbuf, s)
-        acc1[...] += lax.dot_general(xbuf[s], ring[s % SLOTS], LANE_CONTRACT, preferred_element_type=F32)
+        with jax.named_scope('wait1'):
+            tile(s).wait()
+            gather_step(0, xbuf, s)
+        acc1[:100, :] += lax.dot_general(xbuf[s], ring[s % SLOTS], LANE_CONTRACT, preferred_element_type=F32)
         tile(s + SLOTS).start()
         return 0
 
-    lax.fori_loop(0, 16, first, 0)
+    with jax.named_scope('pass1'):
+        lax.fori_loop(0, 16, first, 0)
     for h in range(2):
         sbuf[h] = acc1[:, h * TILE:(h + 1) * TILE].astype(BF16)
     gather_start(1, sbuf, [sbuf.at[h] for h in range(2)])
 
-    acc2[...] = jnp.zeros_like(acc2)
 
     def second(s, _):
-        tile(s + 16).wait()
-        gather_step(1, sbuf, s)
+        with jax.named_scope('wait2'):
+            tile(s + 16).wait()
+            gather_step(1, sbuf, s)
         hid[...] = jnp.maximum(jnp.dot(w1t[...], sbuf[s], preferred_element_type=F32), 0.0).astype(BF16)
         acc2[...] += lax.dot_general(hid[...], ring[s % SLOTS], LANE_CONTRACT, preferred_element_type=F32)
         tile(s + 16 + SLOTS).start()
         return 0
 
-    lax.fori_loop(0, 16, second, 0)
-
-    for c in m_copies:
-        c.wait()
-    count = jnp.sum(jnp.sum(mall[...], axis=0))
+    with jax.named_scope('pass2'):
+        lax.fori_loop(0, 16, second, 0)
+
+    with jax.named_scope('wait_m'):
+        for c in m_copies:
+            c.wait()
+    count = jnp.sum(jnp.sum(mall[...], axis=0).astype(F32))
     classes = lax.broadcasted_iota(jnp.int32, (CLS, 512), 0)
 
     def heads(i, loss):
@@ -137,7 +148,7 @@
         z = z - jnp.max(z, axis=0, keepdims=True)
         logp = z - jnp.log(jnp.sum(jnp.exp(z), axis=0, keepdims=True))
         onehot = (label[:, cols] == classes).astype(F32)
-        weight = mask[:, cols]
+        weight = mask[:, cols].astype(F32)
         g2 = (weight * (jnp.exp(logp) - onehot) / count).astype(BF16)
         dcls[:, cols] = g2
         ut[:, cols] = jnp.dot(w2[...], g2, preferred_element_type=F32).astype(BF16)
@@ -154,9 +165,11 @@
         return remote(cbuf.at[j], rsbuf.at[j], rs_send.at[j], rs_recv.at[j], yn if to_y[j] else xn)
 
     def finalize(j):
-        pair_copy(j).wait_recv()
+        with jax.named_scope('wait_pair'):
+            pair_copy(j).wait_recv()
         if j in (4, 5):
-            link_copy(j - 4).wait_recv()
+            with jax.named_scope('wait_link'):
+                link_copy(j - 4).wait_recv()
             cbuf[j] = (cbuf[j] + rbuf[j]) + rsbuf[j - 4]
         else:
             cbuf[j] = cbuf[j] + rbuf[j]
@@ -186,7 +199,8 @@
                 finalize(jj)
         return 0
 
-    lax.fori_loop(0, 8, third, 0)
+    with jax.named_scope('pass3'):
+        lax.fori_loop(0, 8, third, 0)
     finalize(7)
 
     red[FEAT:FEAT + CLS, :] = lax.dot_general(dcls[...], s2t[...], LANE_CONTRACT, preferred_element_type=F32)
@@ -199,8 +213,9 @@
     dw1 = jnp.zeros((FEAT, HID), F32)
     for h, (a, b) in enumerate(((3, 4), (2, 5))):
         z1 = jnp.dot(w1t[...], sbuf[h], preferred_element_type=F32)
-        link_copy(a).wait_recv()
-        link_copy(b).wait_recv()
+        with jax.named_scope('wait_own'):
+            link_copy(a).wait_recv()
+            link_copy(b).wait_recv()
         g1 = jnp.where(z1 > 0.0, (cbuf[6 + h] + rsbuf[a]) + rsbuf[b], 0.0).astype(BF16)
         dw1 = dw1 + lax.dot_general(sbuf[h], g1, LANE_CONTRACT, preferred_element_type=F32)
     red[:FEAT, :] = dw1
@@ -208,46 +223,55 @@
         link_copy(j).wait_send()
 
     c0 = remote(red, redp, f_send.at[0], f_recv.at[0], partner)
-    c0.start()
-    c0.wait()
+    with jax.named_scope('sum_chip'):
+        c0.start()
+        c0.wait()
     rows = pl.ds(pl.multiple_of(core * (RED // 2), 8), RED // 2)
     half[0] = red[rows, :] + redp[rows, :]
     copies = [remote(half.at[0], half.at[e], f_send.at[e], f_recv.at[e], dev) for e, dev in ((1, xn), (2, yn), (3, diag))]
-    for c in copies:
-        c.start()
-    for c in copies:
-        c.wait()
+    with jax.named_scope('sum_chips'):
+        for c in copies:
+            c.start()
+        for c in copies:
+            c.wait()
     fin[rows, :] = (half[0] + half[1]) + (half[2] + half[3])
     c4 = remote(fin.at[rows], fin.at[rows], f_send.at[4], f_recv.at[4], partner)
-    c4.start()
-    c4.wait()
+    with jax.named_scope('sum_pair'):
+        c4.start()
+        c4.wait()
     out[:FEAT + CLS, :] = fin[:FEAT + CLS, :]
     out[FEAT + CLS:, :] = fin[FEAT + CLS:, :] / count
 
 
+def split(total, loss, dw_one, dw_two_t):
+    loss[...] = total[FEAT + CLS:FEAT + CLS + 1, :1]
+    dw_one[...] = total[:100, :]
+    dw_two_t[...] = total[FEAT:FEAT + 47, :]
+
+
 def solution(mesh):
     vmem, anywhere = pl.BlockSpec(memory_space=pltpu.VMEM), pl.BlockSpec(memory_space=pl.ANY)
 
     def local_step(adj, feat, w_one, w_two, label, mask):
-        feat_t = jnp.pad(feat.T, ((0, FEAT - 100), (0, 0)))
-        w1t = jnp.pad(w_one.astype(BF16).T, ((0, 0), (0, FEAT - 100)))
-        w2 = jnp.pad(w_two.astype(BF16), ((0, 0), (0, 1)))
-        mask_row = mask.astype(F32).reshape(1, ROWS)
+        mask_row = mask.reshape(1, ROWS)
         out = pl.pallas_call(
             kernel,
             out_shape=jax.ShapeDtypeStruct((RED, HID), F32),
-            in_specs=[anywhere, anywhere, vmem, vmem, vmem, vmem, vmem, anywhere],
+            in_specs=[anywhere, anywhere, vmem, vmem, vmem, vmem, anywhere],
             out_specs=vmem,
             scratch_shapes=[
+                pltpu.VMEM((HID, FEAT), BF16),
+                pltpu.VMEM((CLS, HID), BF16),
+                pltpu.VMEM((HID, CLS), BF16),
                 pltpu.VMEM((SLOTS, ROWS, TILE), BF16),
-                pltpu.VMEM((16, FEAT, TILE), BF16),
+                pltpu.VMEM((16, 100, TILE), BF16),
                 pltpu.VMEM((16, FEAT, TILE), BF16),
                 pltpu.VMEM((FEAT, ROWS), F32),
                 pltpu.VMEM((HID, ROWS), F32),
                 pltpu.VMEM((HID, TILE), BF16),
                 pltpu.VMEM((HID, ROWS), BF16),
                 pltpu.VMEM((HID, ROWS), BF16),
-                pltpu.VMEM((8, 1, ROWS), F32),
+                pltpu.VMEM((8, 1, ROWS), jnp.int32),
                 pltpu.VMEM((CLS, ROWS), BF16),
                 pltpu.VMEM((8, HID, TILE), F32),
                 pltpu.VMEM((8, HID, TILE), F32),
@@ -272,7 +296,14 @@
             ],
             compiler_params=pltpu.CompilerParams(collective_id=0, has_side_effects=True, vmem_limit_bytes=67043328),
             name='gcn_step',
-        )(adj, feat_t, w1t, w2.T, w2, label.reshape(1, ROWS), mask_row, mask_row)
-        return (out[FEAT + CLS, :1], out[:100], out[FEAT:FEAT + 47].T)
+        )(adj, feat.T, w_one, w_two.T, label.reshape(1, ROWS), mask_row, mask_row)
+        loss, dw_one, dw_two_t = pl.pallas_call(
+            split,
+            out_shape=[jax.ShapeDtypeStruct(shape, F32) for shape in ((1, 1), (100, HID), (47, HID))],
+            in_specs=[vmem],
+            out_specs=[vmem] * 3,
+            name='split',
+        )(out)
+        return (loss.reshape(1), dw_one, dw_two_t.T)
 
     return jax.shard_map(local_step, mesh=mesh, in_specs=(P('nodes', None), P('nodes', None), P(None, None), P(None, None), P('nodes'), P('nodes')), out_specs=(P(None), P(None, None), P(None, None)), check_vma=False)

time: 127 us -> 117 us (0.921)
  local copies, waits for them, and re-layouts: 7.96 us -> 0 us
  other arithmetic: 2.85 us -> 0 us
    pad x3 -> x0, local copies, waits for them, and re-layouts: 3.06 us -> none  [the longest x1 1.81 us: local_step(): feat_t = jnp.pad(feat.T, ((0, FEAT - 100), (0, 0)))]
    convert_element_type x3 -> x0, other arithmetic: 2.85 us -> none  [the longest x1 1.29 us: local_step(): mask_row = mask.astype(F32).reshape(1, ROWS)]
    slice x2 -> x0, local copies, waits for them, and re-layouts: 2.63 us -> none  [local_step(): return (out[FEAT + CLS, :1], out[:100], out[FEAT:FEAT + 47].T)]
    transpose x2 -> x0, local copies, waits for them, and re-layouts: 2.03 us -> none  [the longest x1 1.35 us: local_step(): return (out[FEAT + CLS, :1], out[:100], out[FEAT:FEAT + 47].T)]
    pallas_call x0 -> x1, Pallas kernels: none -> 1.52 us  [local_step(): pl.pallas_call(split, out_shape=[jax.ShapeDtypeStruct(shape, F32) for sha...]
where the time goes in v2:
time: 117 us
  Pallas kernels  116 us (99%)
    pallas_call x1, Pallas kernels, local_step(): pl.pallas_call(kernel, out_shape=jax.ShapeDtypeStruct((RED, HID), F32), i...  115 us

profile of v2, /device:TPU:0, one launch (start us, length us, event | category | flops | bytes accessed | tf_op | source)
XLA Modules:
  0.0 117.1 jit_solution(2405862745514392932)
XLA Ops:
  0.6 114.9 %gcn_step.1.total = f32[160,128]{1,0:T(8,128)} custom-call(bf16[2048,16384]{1,0:T(8,128)(2,1)} %adj.1, bf16[100,2048]{1,0:T(8,128)(2,1)} %bitcast.6, f32[100,128]{1,0:T(8,128)} %w_one.1, f32[47,128]{1,0:T(8,128)} %bitcast.9, s32[1,2048]{1,0:T(1,128)} %bitcast.10, s32[1,2048]{1,0:T(1,128)} %bitcast.7, s32[1,2048]{1,0:T(1,128)} %bitcast.8), custom_call_target="tpu_custom_call" | custom-call | tf_op jit(solution)/shard_map/gcn_step/pallas_call | solution.py:257
  115.6 1.5 %split.1 = (f32[1,1]{1,0:T(1,128)}, f32[100,128]{1,0:T(8,128)}, f32[47,128]{1,0:T(8,128)}) custom-call(f32[160,128]{1,0:T(8,128)} %gcn_step.1.total), custom_call_target="tpu_custom_call" | custom-call | tf_op jit(solution)/shard_map/split/pallas_call | solution.py:300

commit v3 on v2

--- a/solution.py
+++ b/solution.py
@@ -1,3 +1,5 @@
+import functools
+
 import jax
 import jax.numpy as jnp
 from jax import lax
@@ -12,6 +14,7 @@
 ROWS = 2048
 TILE = 1024
 SLOTS = 8
+FLIP = 1280
 FEAT = 104
 HID = 128
 CLS = 48
@@ -19,7 +22,7 @@
 
 
 def kernel(adj, feat, w_one, w_two_t, label, mask, mask_any, out,
-           w1t, w2t, w2, ring, xbuf, sbuf, acc1, acc2, hid, s2t, ut, mall, dcls,
+           w1t, w2t, w2, ring, flip, xbuf, sbuf, acc1, acc2, hid, s2t, mall, dcls,
            pbuf, rbuf, cbuf, rsbuf, red, redp, half, fin,
            ring_sem, loc_sem, ag_send, ag_recv, m_send, m_recv,
            d_send, d_recv, rs_send, rs_recv, f_send, f_recv):
@@ -33,9 +36,8 @@
 
     def columns(u):
         s, back = u % 16, u // 32
-        g = (1 - back) * (s // 4) + back * (3 - s // 4)
-        r = (1 - back) * (s % 2) + back * ((s // 2) % 2)
-        fc = (1 - back) * ((s // 2) % 2) + back * (1 - s % 2)
+        g, r = (1 - back) * (s // 4) + back * (3 - s // 4), s % 2
+        fc = (back + (s // 2) % 2) % 2
         t = (g + 1) // 2
         fx, fy = (t + 1 - r) // 2, (t + r) // 2
         h = (r + (g // 2) * (3 - g)) % 2
@@ -49,13 +51,12 @@
         return pltpu.make_async_remote_copy(src_ref=src, dst_ref=dst, send_sem=ssem, recv_sem=rsem,
                                             device_id=(dev,), device_id_type=MESH)
 
-    for u in range(SLOTS):
-        tile(u).start()
     own = [pltpu.make_async_copy(feat.at[:, pl.ds(h * TILE, TILE)], xbuf.at[h], loc_sem.at[h]) for h in range(2)]
     own.append(pltpu.make_async_copy(mask_any, mall.at[0], loc_sem.at[2]))
     for c in own:
         c.start()
-
+    for u in range(SLOTS):
+        tile(u).start()
     w1t[...] = jnp.concatenate([w_one[...], jnp.zeros((28, HID), F32)], 0).T[:, :FEAT].astype(BF16)
     wide = jnp.concatenate([w_two_t[...], jnp.zeros((81, HID), F32)], 0)
     w2t[...] = wide[:CLS].astype(BF16)
@@ -105,34 +106,52 @@
     for c in own:
         c.wait()
 
-
-    def first(s, _):
+    def flip_rows(u):
+        return ring[u % SLOTS, :FLIP, :].T
+
+    def pair(acc, rows, x, u):
+        for k in range(2):
+            flip[1 - k] = flip_rows(u + k + 1)
+            acc[:rows, FLIP:] += lax.dot_general(x(k), ring[(u + k) % SLOTS, FLIP:, :], LANE_CONTRACT, preferred_element_type=F32)
+            acc[:rows, :FLIP] += jnp.dot(x(k), flip[k], preferred_element_type=F32)
+
+    tile(0).wait()
+    flip[0] = flip_rows(0)
+
+    def first(i, _):
+        s = 2 * i
         with jax.named_scope('wait1'):
-            tile(s).wait()
-            gather_step(0, xbuf, s)
-        acc1[:100, :] += lax.dot_general(xbuf[s], ring[s % SLOTS], LANE_CONTRACT, preferred_element_type=F32)
-        tile(s + SLOTS).start()
+            for k in range(2):
+                tile(s + k + 1).wait()
+                gather_step(0, xbuf, s + k)
+        pair(acc1, 100, lambda k: xbuf[s + k], s)
+        for k in range(2):
+            tile(s + k + SLOTS).start()
         return 0
 
     with jax.named_scope('pass1'):
-        lax.fori_loop(0, 16, first, 0)
+        lax.fori_loop(0, 8, first, 0)
     for h in range(2):
         sbuf[h] = acc1[:, h * TILE:(h + 1) * TILE].astype(BF16)
     gather_start(1, sbuf, [sbuf.at[h] for h in range(2)])
 
-
-    def second(s, _):
+    def second(i, _):
+        s = 2 * i
         with jax.named_scope('wait2'):
-            tile(s + 16).wait()
-            gather_step(1, sbuf, s)
-        hid[...] = jnp.maximum(jnp.dot(w1t[...], sbuf[s], preferred_element_type=F32), 0.0).astype(BF16)
-        acc2[...] += lax.dot_general(hid[...], ring[s % SLOTS], LANE_CONTRACT, preferred_element_type=F32)
-        tile(s + 16 + SLOTS).start()
+            for k in range(2):
+                tile(s + k + 17).wait()
+                gather_step(1, sbuf, s + k)
+        for k in range(2):
+            hid[:, k * TILE:(k + 1) * TILE] = jnp.maximum(jnp.dot(w1t[...], sbuf[s + k], preferred_element_type=F32), 0.0).astype(BF16)
+        pair(acc2, HID, lambda k: hid[:, k * TILE:(k + 1) * TILE], s + 16)
+        for k in range(2):
+            tile(s + k + 16 + SLOTS).start()
         return 0
 
     with jax.named_scope('pass2'):
-        lax.fori_loop(0, 16, second, 0)
-
+        lax.fori_loop(0, 8, second, 0)
+
+    ut = hid
     with jax.named_scope('wait_m'):
         for c in m_copies:
             c.wait()
@@ -159,7 +178,7 @@
     to_y = (True, False, False, True, False, True)
 
     def pair_copy(j):
-        return remote(pbuf.at[j], rbuf.at[j], d_send.at[j], d_recv.at[j], partner)
+        return remote(pbuf.at[j % 4], rbuf.at[j], d_send.at[j], d_recv.at[j], partner)
 
     def link_copy(j):
         return remote(cbuf.at[j], rsbuf.at[j], rs_send.at[j], rs_recv.at[j], yn if to_y[j] else xn)
@@ -176,38 +195,34 @@
         if j < 6:
             link_copy(j).start()
 
-    def third(j, _):
-        u = 32 + 2 * j
-        tile(u).wait()
-        pbuf[j] = jnp.dot(ut[...], ring[u % SLOTS], preferred_element_type=F32)
-        pair_copy(j).start()
-
-        @pl.when(j < 4)
-        def _():
-            tile(u + SLOTS).start()
-
-        tile(u + 1).wait()
-        cbuf[j] = jnp.dot(ut[...], ring[(u + 1) % SLOTS], preferred_element_type=F32)
-
-        @pl.when(j < 4)
-        def _():
-            tile(u + 1 + SLOTS).start()
-
-        for jj in range(7):
-            @pl.when(j == jj + 1)
-            def _(jj=jj):
-                finalize(jj)
+    def third(k, _):
+        for q in range(4):
+            u, j = 32 + 4 * k + q, 2 * k + q % 2
+            if q == 0:
+                pl.when(k > 0)(tile(u).wait)
+            else:
+                tile(u).wait()
+            term = jnp.dot(ut[...], ring[u % SLOTS], preferred_element_type=F32)
+            if q < 2:
+                pl.when(k >= 2)(pair_copy(j - 4).wait_send)
+                pbuf[j % 4] = term
+                pair_copy(j).start()
+            else:
+                cbuf[j] = term
+            pl.when(k < 2)(tile(u + SLOTS).start)
+            if q >= 2:
+                for kk in range(4):
+                    pl.when(k == kk)(functools.partial(finalize, 2 * kk + q - 2))
         return 0
 
     with jax.named_scope('pass3'):
-        lax.fori_loop(0, 8, third, 0)
-    finalize(7)
+        lax.fori_loop(0, 4, third, 0)
 
     red[FEAT:FEAT + CLS, :] = lax.dot_general(dcls[...], s2t[...], LANE_CONTRACT, preferred_element_type=F32)
     red[FEAT + CLS:, :] = jnp.broadcast_to(-jnp.sum(loss), (8, HID))
     gather_finish(0, xbuf)
     gather_finish(1, sbuf)
-    for j in range(8):
+    for j in range(4, 8):
         pair_copy(j).wait_send()
 
     dw1 = jnp.zeros((FEAT, HID), F32)
@@ -264,16 +279,16 @@
                 pltpu.VMEM((CLS, HID), BF16),
                 pltpu.VMEM((HID, CLS), BF16),
                 pltpu.VMEM((SLOTS, ROWS, TILE), BF16),
+                pltpu.VMEM((2, TILE, FLIP), BF16),
                 pltpu.VMEM((16, 100, TILE), BF16),
                 pltpu.VMEM((16, FEAT, TILE), BF16),
                 pltpu.VMEM((FEAT, ROWS), F32),
                 pltpu.VMEM((HID, ROWS), F32),
-                pltpu.VMEM((HID, TILE), BF16),
                 pltpu.VMEM((HID, ROWS), BF16),
                 pltpu.VMEM((HID, ROWS), BF16),
                 pltpu.VMEM((8, 1, ROWS), jnp.int32),
                 pltpu.VMEM((CLS, ROWS), BF16),
-                pltpu.VMEM((8, HID, TILE), F32),
+                pltpu.VMEM((4, HID, TILE), F32),
                 pltpu.VMEM((8, HID, TILE), F32),
                 pltpu.VMEM((8, HID, TILE), F32),
                 pltpu.VMEM((6, HID, TILE), F32),

time: 117 us -> 103 us (0.88)
  Pallas kernels: 116 us -> 103 us
    pallas_call x1, Pallas kernels: 115 us -> 101 us  [local_step(): pl.pallas_call(kernel, out_shape=jax.ShapeDtypeStruct((RED, HID), F32), i...]
where the time goes in v3:
time: 103 us
  Pallas kernels  103 us (100%)
    pallas_call x1, Pallas kernels, local_step(): pl.pallas_call(kernel, out_shape=jax.ShapeDtypeStruct((RED, HID), F32), i...  101 us

profile of v3, /device:TPU:0, one launch (start us, length us, event | category | flops | bytes accessed | tf_op | source)
XLA Modules:
  0.0 103.2 jit_solution(12101057293750292779)
XLA Ops:
  0.6 101.1 %gcn_step.1.total = f32[160,128]{1,0:T(8,128)} custom-call(bf16[2048,16384]{1,0:T(8,128)(2,1)} %adj.1, bf16[100,2048]{1,0:T(8,128)(2,1)} %bitcast.6, f32[100,128]{1,0:T(8,128)} %w_one.1, f32[47,128]{1,0:T(8,128)} %bitcast.9, s32[1,2048]{1,0:T(1,128)} %bitcast.10, s32[1,2048]{1,0:T(1,128)} %bitcast.7, s32[1,2048]{1,0:T(1,128)} %bitcast.8), custom_call_target="tpu_custom_call" | custom-call | tf_op jit(solution)/shard_map/gcn_step/pallas_call | solution.py:272
  101.7 1.5 %split.1 = (f32[1,1]{1,0:T(1,128)}, f32[100,128]{1,0:T(8,128)}, f32[47,128]{1,0:T(8,128)}) custom-call(f32[160,128]{1,0:T(8,128)} %gcn_step.1.total), custom_call_target="tpu_custom_call" | custom-call | tf_op jit(solution)/shard_map/split/pallas_call | solution.py:315
